TPU v7x, 32 devices: a whole 2x2x4 slice. The times are simulated.
32 devices in a mesh: grp: 2 (over x), path: 8 (over z, y), amp: 2 (over core).
Axes of the slice: x: 2, y: 2, z: 4, core: 2. Of those that a mesh axis runs over, the one named last changes fastest.
Arguments:
- left_slabs: bfloat16 [256, 2, 16384], P(('grp', 'path'), None, 'amp'), parts along dimension 0, may hold values from -0.59765625 to 0.59765625
- right_slabs: bfloat16 [256, 2, 8192], P(('grp', 'path'), None, 'amp'), parts along dimension 0, may hold values from -0.59765625 to 0.59765625
- term_index: int32 [256], P(('grp', 'path')), parts along dimension 0, may hold values from 0 to 3
- left_terms: float32 [4, 2, 2, 2], replicated, may hold values from -4.2 to 4.2
- right_terms: float32 [4, 2, 2, 2], replicated, may hold values from -4.2 to 4.2
- left_gates: bfloat16 [2, 2, 128, 128], replicated, may hold values from -0.375 to 0.375
- right_gates: bfloat16 [2, 2, 128, 128], replicated, may hold values from -0.375 to 0.375
Outputs:
- amplitudes: bfloat16 [2, 32768, 8192], P(None, ('grp', 'path'), 'amp'), parts along dimension 1
There are 2 independent parts, one for each index of `grp`. A program takes and returns all parts, laid end to end along the dimension named above; an argument that names none is the same for every part. Nothing has to cross between parts.
All inputs are finite; a program needn't handle non-finite values.
Results may differ from a plain program's by a relative error of at most 0.0081.
Values may be sent and summed in bfloat16 or wider, within the bound.
No kernel may reach another device: no remote copies, remote signals or barrier semaphores. Data moves between devices by JAX's collectives and lax.ppermute only.
A program may use at most 128 MiB of HBM per device.

v0:
```python
import jax
import jax.numpy as jnp
from jax import lax
from jax.sharding import PartitionSpec as P


def cut_term(slab, term_mix):
    paths_here, _, length = slab.shape
    width = min(128, length)
    values = slab.astype(jnp.float32).reshape(paths_here, 2, length // width, width)
    identity = jnp.eye(width // 2, dtype=jnp.float32)

    def expand(part):
        return jnp.einsum("ab,nmj->najbm", identity, part).reshape(paths_here, width, width)

    real_kron = expand(term_mix[:, 0])
    imag_kron = expand(term_mix[:, 1])
    batch_dims = (((2,), (1,)), ((0,), (0,)))

    def times(rows, kron):
        return lax.dot_general(
            rows,
            kron,
            batch_dims,
            precision=lax.Precision.HIGHEST,
            preferred_element_type=jnp.float32,
        )

    real_rows = values[:, 0]
    imag_rows = values[:, 1]
    real_part = times(real_rows, real_kron) - times(imag_rows, imag_kron)
    imag_part = times(real_rows, imag_kron) + times(imag_rows, real_kron)
    return jnp.stack([real_part, imag_part], 1).reshape(paths_here, 2, length).astype(jnp.bfloat16)


def apply_low(slab, gate_mat):
    paths_here, _, length = slab.shape
    gate_width = gate_mat.shape[-1]
    real_rows = slab[:, 0].reshape(-1, gate_width)
    imag_rows = slab[:, 1].reshape(-1, gate_width)
    upper = jnp.concatenate([gate_mat[0].T, gate_mat[1].T], 1)
    lower = jnp.concatenate([-gate_mat[1].T, gate_mat[0].T], 1)
    right_matrix = jnp.concatenate([upper, lower], 0)
    product = jnp.dot(
        jnp.concatenate([real_rows, imag_rows], 1), right_matrix, preferred_element_type=jnp.float32
    )
    real_part = product[:, :gate_width].reshape(paths_here, length)
    imag_part = product[:, gate_width:].reshape(paths_here, length)
    return jnp.stack([real_part, imag_part], 1).astype(jnp.bfloat16)


def stack_matrix(gate_mat):
    upper = jnp.concatenate([gate_mat[0], -gate_mat[1]], 1)
    lower = jnp.concatenate([gate_mat[1], gate_mat[0]], 1)
    return jnp.concatenate([upper, lower], 0)


def gate_rows(matrix, data):
    batch = jnp.broadcast_to(matrix, (data.shape[0],) + matrix.shape)
    return lax.dot_general(
        batch, data, (((2,), (1,)), ((0,), (0,))), preferred_element_type=jnp.float32
    )


def right_high(moved, gate_mat):
    half_paths = moved.shape[0]
    gate_width = gate_mat.shape[-1]
    low_width = gate_width // 2
    data = moved.reshape(half_paths, gate_width, gate_width)
    blocks = gate_mat.reshape(2, low_width, 2, low_width, 2)
    rows_index = jnp.arange(gate_width, dtype=jnp.int32)[:, None]
    cols_index = jnp.arange(gate_width, dtype=jnp.int32)[None, :]
    same_slot = rows_index % low_width == cols_index % low_width
    total = jnp.zeros((half_paths, gate_width, gate_width), jnp.float32)
    for target in range(2):
        for source in range(2):
            select = (
                same_slot
                & (rows_index // low_width == source)
                & (cols_index // low_width == target)
            ).astype(jnp.bfloat16)
            placed = jnp.dot(
                data.reshape(-1, gate_width), select, preferred_element_type=jnp.float32
            )
            placed = placed.astype(jnp.bfloat16).reshape(half_paths, gate_width, gate_width)
            matrix = stack_matrix(blocks[:, :, target, :, source])
            total = total + gate_rows(matrix, placed)
    return total.astype(jnp.bfloat16).reshape(half_paths, 2, -1)


def contract(left_part, right_part):
    left_stack = jnp.concatenate([left_part[:, 0], left_part[:, 1]], 0)
    right_real = jnp.concatenate([right_part[:, 0], -right_part[:, 1]], 0)
    right_imag = jnp.concatenate([right_part[:, 1], right_part[:, 0]], 0)
    contract_dims = (((0,), (0,)), ((), ()))
    real_part = lax.dot_general(
        left_stack, right_real, contract_dims, preferred_element_type=jnp.float32
    )
    imag_part = lax.dot_general(
        left_stack, right_imag, contract_dims, preferred_element_type=jnp.float32
    )
    return (real_part, imag_part)


def mixes(term_index, terms):
    chosen = (term_index[:, None] == jnp.arange(terms.shape[0], dtype=jnp.int32)[None, :]).astype(
        jnp.float32
    )
    flat = jnp.dot(chosen, terms.reshape(terms.shape[0], 8), precision=lax.Precision.HIGHEST)
    return flat.reshape(-1, 2, 2, 2)


def shards(left_slabs, right_slabs, term_index, left_terms, right_terms, left_gates, right_gates):
    gate_width = left_gates.shape[-1]
    path_count = lax.axis_size("path")
    left = cut_term(left_slabs, mixes(term_index, left_terms))
    left = apply_low(left, left_gates[0])
    moved = lax.all_to_all(left, "amp", split_axis=0, concat_axis=2, tiled=True)
    half_paths = moved.shape[0]
    full_left = moved.shape[2]
    turned = gate_rows(
        stack_matrix(left_gates[1]),
        moved.reshape(half_paths, 2 * gate_width, full_left // gate_width),
    )
    turned = turned.astype(jnp.bfloat16).reshape(half_paths, 2, full_left)
    portion = lax.all_to_all(turned, "path", split_axis=2, concat_axis=0, tiled=True)
    rows_here = portion.shape[2]
    portion = portion.reshape(path_count, half_paths, 2, rows_here)
    row_block = lax.all_gather(portion, "amp", axis=1, tiled=True).reshape(
        path_count * half_paths * 2, 2, rows_here
    )
    right = cut_term(right_slabs, mixes(term_index, right_terms))
    right = apply_low(right, right_gates[0])
    right_moved = lax.all_to_all(right, "amp", split_axis=0, concat_axis=2, tiled=True)
    right_turned = right_high(right_moved, right_gates[1])
    right = lax.all_to_all(right_turned, "amp", split_axis=2, concat_axis=0, tiled=True)
    everything = lax.all_gather(right, "path", axis=0, tiled=True)
    real_part, imag_part = contract(row_block, everything)
    return jnp.stack([real_part, imag_part], 0).astype(jnp.bfloat16)


def solution(mesh):
    return jax.shard_map(
        shards,
        mesh=mesh,
        in_specs=(
            P(("grp", "path"), None, "amp"),
            P(("grp", "path"), None, "amp"),
            P(("grp", "path")),
            P(),
            P(),
            P(),
            P(),
        ),
        out_specs=P(None, ("grp", "path"), "amp"),
        check_vma=False,
    )
```

profile of v0, /device:TPU:0, one launch (start us, length us, event | category | flops | bytes accessed | tf_op | source)
XLA Modules:
  0.0 288.8 jit_solution(7753225383539384605)
XLA Ops:
  7.3 0.8 slice_bitcast_fusion.20
  9.0 0.8 fusion.66
  9.8 1.4 reshape.234
  11.3 18.8 %broadcast_multiply_fusion.3 = (f32[16,2,2,64,64]{0,1,4,2,3:T(2,128)}, f32[16,2,2,64,64]{0,1,4,2,3:T(2,128)}, f32[16,2,2,64,64]{0,1,4,2,3:T(2,128)}, f32[16,2,2,64,64]{0,1,4,2,3:T(2,128)}) fusion(f32[64,64]{1,0:T(8,128)S(1)} %fusion.61, f32[16,2,2]{0,1,2:T(2,128)S(1)} %copy.56, f32[16,2,2]{0,1,2:T(2,128)S(1)} %copy.59, f32[16,2,2]{0,1,2:T(2,128)S(1)} %copy.69, ...), kind=kLoop, calls=%fused_computation.6 | loop fusion | flops 1048576 | bytes 4211712 | tf_op jit(solution)/shard_map/ab,nmj->najbm/dot_general | solution.py:14
  30.1 5.2 %copy.58 = f32[16,128,128]{2,1,0:T(8,128)S(1)} copy(f32[16,128,128]{0,2,1:T(8,128)} %bitcast.165) | data formatting | bytes 2097152 | tf_op jit(solution)/shard_map/reshape | solution.py:14
  35.3 5.2 %copy.60 = f32[16,128,128]{2,1,0:T(8,128)S(1)} copy(f32[16,128,128]{0,2,1:T(8,128)} %bitcast.164) | data formatting | bytes 2097152 | tf_op jit(solution)/shard_map/reshape | solution.py:14
  43.8 2.0 pad_maximum_fusion.4
  45.8 3.7 %all-to-all-start = ((bf16[16,2,8192]{2,1,0:T(2,128)(2,1)}), bf16[16,2,8192]{2,1,0:T(2,128)(2,1)S(1)}, u32[]{:S(2)}, u32[]{:S(2)}) async-start(bf16[16,2,8192]{2,1,0:T(2,128)(2,1)} %pad_maximum_fusion.4), calls=%async_computation | async-start | bytes 1048576 | tf_op jit(solution)/shard_map/all_to_all | solution.py:118
  50.5 10.0 %reshape_squeeze.17 = bf16[2,64,2,64,2]{4,3,2,1,0:T(8,128)(2,1)} reshape(bf16[1,2,128,128]{3,2,1,0:T(8,128)(2,1)S(1)} %slice-done) | data formatting | bytes 131072 | tf_op jit(solution)/shard_map/reshape;squeeze | solution.py:70
  60.5 7.9 %slice_reduce_fusion = (bf16[64,64]{1,0:T(8,128)(2,1)S(1)}, bf16[64,64]{1,0:T(8,128)(2,1)S(1)}, bf16[64,64]{1,0:T(8,128)(2,1)S(1)}, bf16[64,64]{1,0:T(8,128)(2,1...) fusion(bf16[2,64,2,64,2]{4,3,2,1,0:T(8,128)(2,1)} %reshape_sque, ...), kind=kLoop, calls=%fused_computation.34 | loop fusion | bytes 131072 | tf_op jit(solution)/shard_map/slice | solution.py:53
  68.5 5.2 %copy.71 = f32[16,128,128]{2,1,0:T(8,128)S(1)} copy(f32[16,128,128]{0,2,1:T(8,128)} %bitcast.163) | data formatting | bytes 2097152 | tf_op jit(solution)/shard_map/reshape | solution.py:14
  73.8 5.2 %copy.73 = f32[16,128,128]{2,1,0:T(8,128)S(1)} copy(f32[16,128,128]{0,2,1:T(8,128)} %bitcast.162) | data formatting | bytes 2097152 | tf_op jit(solution)/shard_map/reshape | solution.py:14
  81.9 1.3 pad_maximum_fusion.5
  83.2 3.4 %all-to-all-start.2 = ((bf16[16,2,4096]{2,1,0:T(2,128)(2,1)}), bf16[16,2,4096]{2,1,0:T(2,128)(2,1)S(1)}, u32[]{:S(2)}, u32[]{:S(2)}) async-start(bf16[16,2,4096]{2,1,0:T(2,128)(2,1)} %pad_maximum_fusion.5), calls=%async_computation.2 | async-start | bytes 524288 | tf_op jit(solution)/shard_map/all_to_all | solution.py:134
  88.2 12.8 %copy.66 = bf16[8,2,16384]{0,1,2:T(2,128)(2,1)} copy(bf16[8,2,16384]{2,1,0:T(2,128)(2,1)S(1)} %reshape.222) | data formatting | bytes 1048576 | tf_op jit(solution)/shard_map/reshape | solution.py:125
  100.9 11.1 %reshape.246 = bf16[8,2,16384]{2,1,0:T(2,128)(2,1)} reshape(bf16[16384,2,8]{2,1,0:T(2,128)(2,1)} %bitcast.160) | data formatting | bytes 1048576
  112.1 7.3 %all-to-all-start.1 = ((bf16[8,2,16384]{2,1,0:T(2,128)(2,1)}), bf16[8,2,16384]{2,1,0:T(2,128)(2,1)S(1)}, u32[]{:S(2)}, u32[]{:S(2)}) async-start(bf16[8,2,16384]{2,1,0:T(2,128)(2,1)} %reshape.246), calls=%async_computation.1 | async-start | bytes 1048576 | tf_op jit(solution)/shard_map/all_to_all | solution.py:126
  121.6 12.9 %all-to-all-done.1 = bf16[8,2,16384]{2,1,0:T(2,128)(2,1)S(1)} async-done(((bf16[8,2,16384]{2,1,0:T(2,128)(2,1)}), bf16[8,2,16384]{2,1,0:T(2,128)(2,1)S(1)}, u32[]{:S(2)}, u32[]{:S(2)}) %all-to-all-start.1) | async-done | bytes 524320 | tf_op jit(solution)/shard_map/all_to_all | solution.py:126
  134.5 10.9 %reshape.247 = bf16[16384,2,8]{2,1,0:T(2,128)(2,1)} reshape(bf16[8,2,16384]{2,1,0:T(2,128)(2,1)S(1)} %all-to-all-done.1) | data formatting | bytes 1048576
  145.4 12.5 %copy.85 = bf16[8,2,8,2048]{3,2,0,1:T(8,128)(2,1)} copy(bf16[8,2,8,2048]{0,1,3,2:T(2,128)(2,1)} %bitcast.161) | data formatting | bytes 1048576 | tf_op jit(solution)/shard_map/all_to_all | solution.py:126
  159.1 6.8 %copy.80 = bf16[8,2,8192]{0,1,2:T(2,128)(2,1)} copy(bf16[8,2,8192]{2,1,0:T(2,128)(2,1)S(1)} %reshape.232) | data formatting | bytes 524288 | tf_op jit(solution)/shard_map/reshape | solution.py:88
  165.9 6.1 %reshape.244 = bf16[2,2,32768]{2,1,0:T(2,128)(2,1)S(1)} reshape(bf16[8192,2,8]{2,1,0:T(2,128)(2,1)} %bitcast.166) | data formatting | bytes 524288
  172.0 3.9 %all_to_all.63 = bf16[2,2,32768]{2,1,0:T(2,128)(2,1)S(1)} all-to-all(bf16[2,2,32768]{2,1,0:T(2,128)(2,1)S(1)} %reshape.244), channel_id=1, replica_groups=mesh['grp'=2,'path'=8,'amp'=2] {'amp'}, dimensions={0} | all-to-all | bytes 524288 | tf_op jit(solution)/shard_map/all_to_all | solution.py:136
  175.9 6.2 %reshape.245 = bf16[8192,2,8]{2,1,0:T(2,128)(2,1)} reshape(bf16[2,2,32768]{2,1,0:T(2,128)(2,1)S(1)} %all_to_all.63) | data formatting | bytes 524288
  182.1 9.3 %copy.82 = bf16[2,8,2,4096]{3,1,0,2:T(8,128)(2,1)} copy(bf16[2,8,2,4096]{1,2,3,0:T(2,128)(2,1)} %bitcast.167) | data formatting | bytes 524288 | tf_op jit(solution)/shard_map/all_to_all | solution.py:136
  191.4 1.8 copy.68
  193.4 46.4 %all-gather.5.cloned.1.call-done = bf16[128,2,4096]{2,0,1:T(8,128)(2,1)} async-done(((bf16[16,2,4096]{2,0,1:T(8,128)(2,1)}), bf16[128,2,4096]{2,0,1:T(8,128)(2,1)}) %all-gather.5.cloned.1.call-update) | async-done | bytes 2097168 | tf_op jit(solution)/shard_map/all_gather | solution.py:137
  239.8 1.7 slice_bitcast_fusion
  241.5 8.1 %convert_bitcast_fusion = bf16[1,2048,4096]{2,1,0:T(8,128)(2,1)} fusion(bf16[128,4096]{1,0:T(8,128)(2,1)S(1)} %get-tuple-element.14, bf16[128,4096]{1,0:T(8,128)(2,1)S(1)} %get-tuple-element.13, bf16[128,2048]{1,0:T(8,128)(2,1)S(1)} %get-tuple-element.16, bf16[128,2048]{1,0:T(8,128)(2,1)S(1)} %get-tuple-element.15), kind=kOutput, calls=%fused_computation.1 | convolution fusion | flops 4309647360 | bytes 19922944 | tf_op jit(solution)/shard_map/dot_general | solution.py:99
  249.6 1.3 fusion.82
  250.9 8.1 %convert_bitcast_fusion.1 = bf16[1,2048,4096]{2,1,0:T(8,128)(2,1)} fusion(bf16[128,4096]{1,0:T(8,128)(2,1)S(1)} %fusion.82, bf16[128,4096]{1,0:T(8,128)(2,1)S(1)} %get-tuple-element.14, bf16[128,2048]{1,0:T(8,128)(2,1)S(1)} %get-tuple-element.16, bf16[128,2048]{1,0:T(8,128)(2,1)S(1)} %get-tuple-element.15), kind=kOutput, calls=%fused_computation.2 | convolution fusion | flops 4309647360 | bytes 19922944 | tf_op jit(solution)/shard_map/dot_general | solution.py:96
  259.0 23.0 %pad_maximum_fusion = bf16[2,2048,4096]{2,1,0:T(8,128)(2,1)} fusion(bf16[1,2048,4096]{2,1,0:T(8,128)(2,1)} %convert_bitcast_fusion, bf16[1,2048,4096]{2,1,0:T(8,128)(2,1)} %convert_bitcast_fusion.1), kind=kLoop, calls=%fused_computation | loop fusion | flops 16777216 | bytes 67108864 | tf_op jit(solution)/shard_map/stack | solution.py:139
  (72 shorter events, 13.5 us)
Async XLA Ops:
  6.5 1.6 copy-start
  40.6 9.7 %copy-start.2 = (bf16[2,2,128,128]{3,2,1,0:T(8,128)(2,1)S(1)}, bf16[2,2,128,128]{3,2,1,0:T(8,128)(2,1)}, u32[]{:S(2)}) copy-start(bf16[2,2,128,128]{3,2,1,0:T(8,128)(2,1)} %param.13) | copy-start | bytes 393220
  40.6 9.7 %copy-start.3 = (bf16[16,2,4096]{2,1,0:T(2,128)(2,1)S(1)}, bf16[16,2,4096]{2,1,0:T(2,128)(2,1)}, u32[]{:S(2)}) copy-start(bf16[16,2,4096]{2,1,0:T(2,128)(2,1)} %param.8) | copy-start | bytes 786436
  40.6 9.9 %slice-start = ((bf16[2,2,128,128]{3,2,1,0:T(8,128)(2,1)}), bf16[1,2,128,128]{3,2,1,0:T(8,128)(2,1)S(1)}, s32[]{:S(2)}) async-start(bf16[2,2,128,128]{3,2,1,0:T(8,128)(2,1)} %param.13), calls=%async_computation.6 | async-start | bytes 131072 | tf_op jit(solution)/shard_map/slice | solution.py:135
  45.8 37.4 %all-to-all-start = ((bf16[16,2,8192]{2,1,0:T(2,128)(2,1)}), bf16[16,2,8192]{2,1,0:T(2,128)(2,1)S(1)}, u32[]{:S(2)}, u32[]{:S(2)}) async-start(bf16[16,2,8192]{2,1,0:T(2,128)(2,1)} %pad_maximum_fusion.4), calls=%async_computation | async-start | bytes 1048576 | tf_op jit(solution)/shard_map/all_to_all | solution.py:118
  83.2 28.9 %all-to-all-start.2 = ((bf16[16,2,4096]{2,1,0:T(2,128)(2,1)}), bf16[16,2,4096]{2,1,0:T(2,128)(2,1)S(1)}, u32[]{:S(2)}, u32[]{:S(2)}) async-start(bf16[16,2,4096]{2,1,0:T(2,128)(2,1)} %pad_maximum_fusion.5), calls=%async_computation.2 | async-start | bytes 524288 | tf_op jit(solution)/shard_map/all_to_all | solution.py:134
  112.1 22.5 %all-to-all-start.1 = ((bf16[8,2,16384]{2,1,0:T(2,128)(2,1)}), bf16[8,2,16384]{2,1,0:T(2,128)(2,1)S(1)}, u32[]{:S(2)}, u32[]{:S(2)}) async-start(bf16[8,2,16384]{2,1,0:T(2,128)(2,1)} %reshape.246), calls=%async_computation.1 | async-start | bytes 1048576 | tf_op jit(solution)/shard_map/all_to_all | solution.py:126
  119.4 72.0 %all-gather.3.cloned.1.call-start = ((), (), s32[]{:S(2)}) async-start(), calls=%async_computation.4 | async-start | bytes 1572864 | tf_op jit(solution)/shard_map/all_gather | solution.py:129
  158.0 81.8 %all-gather.5.cloned.1.call-start = ((), (), s32[]{:S(2)}) async-start(), calls=%async_computation.5 | async-start | bytes 2359296 | tf_op jit(solution)/shard_map/all_gather | solution.py:137
  259.0 23.0 %copy-start.1 = (f32[4,2,2,2]{0,3,2,1:T(2,128)S(1)}, f32[4,2,2,2]{0,3,2,1:T(2,128)}, u32[]{:S(2)}) copy-start(f32[4,2,2,2]{0,3,2,1:T(2,128)} %param.10) | copy-start | bytes 388
Sparse Core Ops, SparseCore 0:
  158.1 8.0 all-gather.2
  191.5 48.2 all-gather.4
where the time goes:
time: 290 us; the launch traced here: 289 us
  local copies, waits for them, and re-layouts  123 us (42%)
  waiting for transfers between devices  59.4 us (20%)
  other arithmetic  48.2 us (17%)
  matrix products  25.9 us (9%)
  starting transfers between devices  14.7 us (5%)
  between operations  13.9 us (5%)
  blocking collectives  3.94 us (1%)
    all_gather x1, waiting for transfers between devices, shards(): everything = lax.all_gather(right, 'path', axis=0, tiled=True)  46.4 us
    unnamed x12, local copies, waits for them, and re-layouts  34.3 us
    another operation x1, other arithmetic, shards(): return jnp.stack([real_part, imag_part], 0).astype(jnp.bfloat16)  23 us
    reshape x4, local copies, waits for them, and re-layouts, expand(): jnp.einsum('ab,nmj->najbm', identity, part)  20.9 us
    dot_general x1, other arithmetic, expand(): jnp.einsum('ab,nmj->najbm', identity, part)  18.8 us
    reshape x2, local copies, waits for them, and re-layouts, shards(): turned = turned.astype(jnp.bfloat16).reshape(half_paths, 2, full_left)  12.9 us
    all_to_all x1, waiting for transfers between devices, shards(): lax.all_to_all(turned, 'path', split_axis=2, concat_axis=0, tiled=True)  12.9 us
    all_to_all x1, local copies, waits for them, and re-layouts, shards(): lax.all_to_all(turned, 'path', split_axis=2, concat_axis=0, tiled=True)  12.5 us
  transfers between devices with their start and end apart: 5, of which 2 were waited for; matrix products, arithmetic and copies ran while one was open for 32% of the time, Pallas kernels for 0%

commit v1 on v0

--- a/solution.py
+++ b/solution.py
@@ -123,7 +123,9 @@
         moved.reshape(half_paths, 2 * gate_width, full_left // gate_width),
     )
     turned = turned.astype(jnp.bfloat16).reshape(half_paths, 2, full_left)
-    portion = lax.all_to_all(turned, "path", split_axis=2, concat_axis=0, tiled=True)
+    pieces = jnp.split(turned, lax.axis_size("path"), axis=2)
+    arrived = lax.all_to_all(jnp.stack(pieces), "path", 0, 0)
+    portion = jnp.concatenate(arrived, axis=0)
     rows_here = portion.shape[2]
     portion = portion.reshape(path_count, half_paths, 2, rows_here)
     row_block = lax.all_gather(portion, "amp", axis=1, tiled=True).reshape(

time: 290 us -> 249 us (0.86)
  local copies, waits for them, and re-layouts: 123 us -> 81.4 us
    unnamed x12 -> x19, local copies, waits for them, and re-layouts: 34.3 us -> 17.8 us
    reshape x2 -> x1, local copies, waits for them, and re-layouts: 12.9 us -> 0.12 us  [shards(): turned = turned.astype(jnp.bfloat16).reshape(half_paths, 2, full_left)]
    all_to_all x1 -> x0, local copies, waits for them, and re-layouts: 12.5 us -> none  [shards(): lax.all_to_all(turned, 'path', split_axis=2, concat_axis=0, tiled=True)]
  transfers between devices with their start and end apart: 5 -> 5, of which waited for: 2 -> 2; matrix products, arithmetic and copies ran while one was open for 32% -> 30% of each run, Pallas kernels for 0% -> 0%
where the time goes in v1:
time: 249 us; the launch traced here: 248 us
  local copies, waits for them, and re-layouts  81.4 us (33%)
  waiting for transfers between devices  59.6 us (24%)
  other arithmetic  48.2 us (19%)
  matrix products  26.1 us (10%)
  starting transfers between devices  14.7 us (6%)
  between operations  13.9 us (6%)
  blocking collectives  3.94 us (2%)
    all_gather x1, waiting for transfers between devices, shards(): everything = lax.all_gather(right, 'path', axis=0, tiled=True)  46.6 us
    another operation x1, other arithmetic, shards(): return jnp.stack([real_part, imag_part], 0).astype(jnp.bfloat16)  23 us
    reshape x4, local copies, waits for them, and re-layouts, expand(): jnp.einsum('ab,nmj->najbm', identity, part)  20.9 us
    dot_general x1, other arithmetic, expand(): jnp.einsum('ab,nmj->najbm', identity, part)  18.8 us
    unnamed x19, local copies, waits for them, and re-layouts  17.8 us
    all_to_all x1, waiting for transfers between devices, shards(): arrived = lax.all_to_all(jnp.stack(pieces), 'path', 0, 0)  12.9 us
    another operation x1, local copies, waits for them, and re-layouts, right_high(): blocks = gate_mat.reshape(2, low_width, 2, low_width, 2)  10 us
    all_to_all x1, local copies, waits for them, and re-layouts, shards(): lax.all_to_all(right_turned, 'amp', split_axis=2, concat_axis=0, tiled=True)  9.3 us
  transfers between devices with their start and end apart: 5, of which 2 were waited for; matrix products, arithmetic and copies ran while one was open for 30% of the time, Pallas kernels for 0%

profile of v1, /device:TPU:0, one launch (start us, length us, event | category | flops | bytes accessed | tf_op | source)
XLA Modules:
  0.0 247.9 jit_solution(8860731851766736026)
XLA Ops:
  6.5 0.8 fusion.88
  7.3 0.8 slice_bitcast_fusion.28
  8.1 0.8 fusion.76
  9.0 0.8 fusion.74
  9.8 1.4 reshape.232
  11.3 18.8 %broadcast_multiply_fusion.3 = (f32[16,2,2,64,64]{0,1,4,2,3:T(2,128)}, f32[16,2,2,64,64]{0,1,4,2,3:T(2,128)}, f32[16,2,2,64,64]{0,1,4,2,3:T(2,128)}, f32[16,2,2,64,64]{0,1,4,2,3:T(2,128)}) fusion(f32[64,64]{1,0:T(8,128)S(1)} %fusion.69, f32[16,2,2]{0,1,2:T(2,128)S(1)} %copy.56, f32[16,2,2]{0,1,2:T(2,128)S(1)} %copy.59, f32[16,2,2]{0,1,2:T(2,128)S(1)} %copy.67, ...), kind=kLoop, calls=%fused_computation.6 | loop fusion | flops 1048576 | bytes 4211712 | tf_op jit(solution)/shard_map/ab,nmj->najbm/dot_general | solution.py:14
  30.1 5.2 %copy.58 = f32[16,128,128]{2,1,0:T(8,128)S(1)} copy(f32[16,128,128]{0,2,1:T(8,128)} %bitcast.191) | data formatting | bytes 2097152 | tf_op jit(solution)/shard_map/reshape | solution.py:14
  35.3 5.2 %copy.60 = f32[16,128,128]{2,1,0:T(8,128)S(1)} copy(f32[16,128,128]{0,2,1:T(8,128)} %bitcast.190) | data formatting | bytes 2097152 | tf_op jit(solution)/shard_map/reshape | solution.py:14
  43.8 2.0 pad_maximum_fusion.4
  45.8 3.7 %all-to-all-start = ((bf16[16,2,8192]{2,1,0:T(2,128)(2,1)}), bf16[16,2,8192]{2,1,0:T(2,128)(2,1)S(1)}, u32[]{:S(2)}, u32[]{:S(2)}) async-start(bf16[16,2,8192]{2,1,0:T(2,128)(2,1)} %pad_maximum_fusion.4), calls=%async_computation | async-start | bytes 1048576 | tf_op jit(solution)/shard_map/all_to_all | solution.py:118
  49.5 0.8 fusion.87
  50.5 10.0 %reshape_squeeze.17 = bf16[2,64,2,64,2]{4,3,2,1,0:T(8,128)(2,1)} reshape(bf16[1,2,128,128]{3,2,1,0:T(8,128)(2,1)S(1)} %slice-done) | data formatting | bytes 131072 | tf_op jit(solution)/shard_map/reshape;squeeze | solution.py:70
  60.6 7.9 %slice_reduce_fusion = (bf16[64,64]{1,0:T(8,128)(2,1)S(1)}, bf16[64,64]{1,0:T(8,128)(2,1)S(1)}, bf16[64,64]{1,0:T(8,128)(2,1)S(1)}, bf16[64,64]{1,0:T(8,128)(2,1...) fusion(bf16[2,64,2,64,2]{4,3,2,1,0:T(8,128)(2,1)} %reshape_sque, ...), kind=kLoop, calls=%fused_computation.34 | loop fusion | bytes 131072 | tf_op jit(solution)/shard_map/slice | solution.py:53
  68.6 5.2 %copy.69 = f32[16,128,128]{2,1,0:T(8,128)S(1)} copy(f32[16,128,128]{0,2,1:T(8,128)} %bitcast.189) | data formatting | bytes 2097152 | tf_op jit(solution)/shard_map/reshape | solution.py:14
  73.8 5.2 %copy.71 = f32[16,128,128]{2,1,0:T(8,128)S(1)} copy(f32[16,128,128]{0,2,1:T(8,128)} %bitcast.188) | data formatting | bytes 2097152 | tf_op jit(solution)/shard_map/reshape | solution.py:14
  81.9 1.3 pad_maximum_fusion.5
  83.2 3.4 %all-to-all-start.2 = ((bf16[16,2,4096]{2,1,0:T(2,128)(2,1)}), bf16[16,2,4096]{2,1,0:T(2,128)(2,1)S(1)}, u32[]{:S(2)}, u32[]{:S(2)}) async-start(bf16[16,2,4096]{2,1,0:T(2,128)(2,1)} %pad_maximum_fusion.5), calls=%async_computation.2 | async-start | bytes 524288 | tf_op jit(solution)/shard_map/all_to_all | solution.py:136
  93.6 7.3 %all-to-all-start.1 = ((bf16[8,8,2,2048]{3,2,1,0:T(2,128)(2,1)}), bf16[8,8,2,2048]{3,2,1,0:T(2,128)(2,1)S(1)}, u32[]{:S(2)}, u32[]{:S(2)}) async-start(bf16[8,8,2,2048]{3,2,1,0:T(2,128)(2,1)} %fusion.45), calls=%async_computation.1 | async-start | bytes 1048576 | tf_op jit(solution)/shard_map/all_to_all | solution.py:127
  103.1 12.9 %all-to-all-done.1 = bf16[8,8,2,2048]{3,2,1,0:T(2,128)(2,1)S(1)} async-done(((bf16[8,8,2,2048]{3,2,1,0:T(2,128)(2,1)}), bf16[8,8,2,2048]{3,2,1,0:T(2,128)(2,1)S(1)}, u32[]{:S(2)}, u32[]{:S(2)}) %all-to-all-start.1) | async-done | bytes 524320 | tf_op jit(solution)/shard_map/all_to_all | solution.py:127
  116.0 0.8 copy-done.2
  118.0 6.8 %copy.78 = bf16[8,2,8192]{0,1,2:T(2,128)(2,1)} copy(bf16[8,2,8192]{2,1,0:T(2,128)(2,1)S(1)} %reshape.230) | data formatting | bytes 524288 | tf_op jit(solution)/shard_map/reshape | solution.py:88
  124.7 6.1 %reshape.242 = bf16[2,2,32768]{2,1,0:T(2,128)(2,1)S(1)} reshape(bf16[8192,2,8]{2,1,0:T(2,128)(2,1)} %bitcast.192) | data formatting | bytes 524288
  130.9 3.9 %all_to_all.53 = bf16[2,2,32768]{2,1,0:T(2,128)(2,1)S(1)} all-to-all(bf16[2,2,32768]{2,1,0:T(2,128)(2,1)S(1)} %reshape.242), channel_id=1, replica_groups=mesh['grp'=2,'path'=8,'amp'=2] {'amp'}, dimensions={0} | all-to-all | bytes 524288 | tf_op jit(solution)/shard_map/all_to_all | solution.py:138
  134.8 6.2 %reshape.243 = bf16[8192,2,8]{2,1,0:T(2,128)(2,1)} reshape(bf16[2,2,32768]{2,1,0:T(2,128)(2,1)S(1)} %all_to_all.53) | data formatting | bytes 524288
  141.0 9.3 %copy.80 = bf16[2,8,2,4096]{3,1,0,2:T(8,128)(2,1)} copy(bf16[2,8,2,4096]{1,2,3,0:T(2,128)(2,1)} %bitcast.193) | data formatting | bytes 524288 | tf_op jit(solution)/shard_map/all_to_all | solution.py:138
  150.3 1.6 copy.66
  152.0 46.6 %all-gather.5.cloned.1.call-done = bf16[128,2,4096]{2,0,1:T(8,128)(2,1)} async-done(((bf16[16,2,4096]{2,0,1:T(8,128)(2,1)}), bf16[128,2,4096]{2,0,1:T(8,128)(2,1)}) %all-gather.5.cloned.1.call-update) | async-done | bytes 2097168 | tf_op jit(solution)/shard_map/all_gather | solution.py:139
  198.7 1.7 slice_bitcast_fusion
  200.3 8.2 %convert_bitcast_fusion = bf16[1,2048,4096]{2,1,0:T(8,128)(2,1)} fusion(bf16[128,4096]{1,0:T(8,128)(2,1)S(1)} %get-tuple-element.14, bf16[128,4096]{1,0:T(8,128)(2,1)S(1)} %get-tuple-element.13, bf16[128,2048]{1,0:T(8,128)(2,1)S(1)} %get-tuple-element.16, bf16[128,2048]{1,0:T(8,128)(2,1)S(1)} %get-tuple-element.15), kind=kOutput, calls=%fused_computation.1 | convolution fusion | flops 4309647360 | bytes 19922944 | tf_op jit(solution)/shard_map/dot_general | solution.py:99
  208.5 1.3 fusion.90
  209.8 8.2 %convert_bitcast_fusion.1 = bf16[1,2048,4096]{2,1,0:T(8,128)(2,1)} fusion(bf16[128,4096]{1,0:T(8,128)(2,1)S(1)} %fusion.90, bf16[128,4096]{1,0:T(8,128)(2,1)S(1)} %get-tuple-element.14, bf16[128,2048]{1,0:T(8,128)(2,1)S(1)} %get-tuple-element.16, bf16[128,2048]{1,0:T(8,128)(2,1)S(1)} %get-tuple-element.15), kind=kOutput, calls=%fused_computation.2 | convolution fusion | flops 4309647360 | bytes 19922944 | tf_op jit(solution)/shard_map/dot_general | solution.py:96
  218.1 23.0 %pad_maximum_fusion = bf16[2,2048,4096]{2,1,0:T(8,128)(2,1)} fusion(bf16[1,2048,4096]{2,1,0:T(8,128)(2,1)} %convert_bitcast_fusion, bf16[1,2048,4096]{2,1,0:T(8,128)(2,1)} %convert_bitcast_fusion.1), kind=kLoop, calls=%fused_computation | loop fusion | flops 16777216 | bytes 67108864 | tf_op jit(solution)/shard_map/stack | solution.py:141
  (78 shorter events, 16.6 us)
Async XLA Ops:
  6.5 1.6 copy-start
  42.5 7.8 %copy-start.3 = (bf16[2,2,128,128]{3,2,1,0:T(8,128)(2,1)S(1)}, bf16[2,2,128,128]{3,2,1,0:T(8,128)(2,1)}, u32[]{:S(2)}) copy-start(bf16[2,2,128,128]{3,2,1,0:T(8,128)(2,1)} %param.13) | copy-start | bytes 393220
  42.5 7.8 %copy-start.4 = (bf16[16,2,4096]{2,1,0:T(2,128)(2,1)S(1)}, bf16[16,2,4096]{2,1,0:T(2,128)(2,1)}, u32[]{:S(2)}) copy-start(bf16[16,2,4096]{2,1,0:T(2,128)(2,1)} %param.8) | copy-start | bytes 786436
  43.1 7.4 %slice-start = ((bf16[2,2,128,128]{3,2,1,0:T(8,128)(2,1)}), bf16[1,2,128,128]{3,2,1,0:T(8,128)(2,1)S(1)}, s32[]{:S(2)}) async-start(bf16[2,2,128,128]{3,2,1,0:T(8,128)(2,1)} %param.13), calls=%async_computation.6 | async-start | bytes 131072 | tf_op jit(solution)/shard_map/slice | solution.py:137
  45.8 37.4 %all-to-all-start = ((bf16[16,2,8192]{2,1,0:T(2,128)(2,1)}), bf16[16,2,8192]{2,1,0:T(2,128)(2,1)S(1)}, u32[]{:S(2)}, u32[]{:S(2)}) async-start(bf16[16,2,8192]{2,1,0:T(2,128)(2,1)} %pad_maximum_fusion.4), calls=%async_computation | async-start | bytes 1048576 | tf_op jit(solution)/shard_map/all_to_all | solution.py:118
  83.2 10.4 %all-to-all-start.2 = ((bf16[16,2,4096]{2,1,0:T(2,128)(2,1)}), bf16[16,2,4096]{2,1,0:T(2,128)(2,1)S(1)}, u32[]{:S(2)}, u32[]{:S(2)}) async-start(bf16[16,2,4096]{2,1,0:T(2,128)(2,1)} %pad_maximum_fusion.5), calls=%async_computation.2 | async-start | bytes 524288 | tf_op jit(solution)/shard_map/all_to_all | solution.py:136
  93.6 22.5 %all-to-all-start.1 = ((bf16[8,8,2,2048]{3,2,1,0:T(2,128)(2,1)}), bf16[8,8,2,2048]{3,2,1,0:T(2,128)(2,1)S(1)}, u32[]{:S(2)}, u32[]{:S(2)}) async-start(bf16[8,8,2,2048]{3,2,1,0:T(2,128)(2,1)} %fusion.45), calls=%async_computation.1 | async-start | bytes 1048576 | tf_op jit(solution)/shard_map/all_to_all | solution.py:127
  100.9 49.4 %all-gather.3.cloned.1.call-start = ((), (), s32[]{:S(2)}) async-start(), calls=%async_computation.4 | async-start | bytes 1572864 | tf_op jit(solution)/shard_map/all_gather | solution.py:131
  116.0 0.8 copy-start.2
  116.9 81.8 %all-gather.5.cloned.1.call-start = ((), (), s32[]{:S(2)}) async-start(), calls=%async_computation.5 | async-start | bytes 2359296 | tf_op jit(solution)/shard_map/all_gather | solution.py:139
  218.1 23.0 %copy-start.1 = (f32[4,2,2,2]{0,3,2,1:T(2,128)S(1)}, f32[4,2,2,2]{0,3,2,1:T(2,128)}, u32[]{:S(2)}) copy-start(f32[4,2,2,2]{0,3,2,1:T(2,128)} %param.10) | copy-start | bytes 388
Sparse Core Ops, SparseCore 0:
  117.0 8.0 all-gather.2
  150.4 48.2 all-gather.4
